TPU v7x, 32 devices: a whole 2x2x4 slice. The times are simulated.
32 devices in a mesh: row: 4 (over z), col: 8 (over y, x, core).
Axes of the slice: x: 2, y: 2, z: 4, core: 2. Of those that a mesh axis runs over, the one named last changes fastest.
Arguments:
- a_matrix: float32 [8192, 8192], P('row', 'col'), may hold values from -14 to 30, as said below
- b_matrix: float32 [4096, 4096], P('row', 'col'), may hold values from -14 to 30, as said below
- c_matrix: float32 [8192, 4096], P('row', 'col'), may hold values from -6 to 6
Outputs:
- a_swept: float32 [8192, 8192], P('row', 'col')
- c_swept: float32 [8192, 4096], P('row', 'col')
- b_next: float32 [4096, 4096], P('row', 'col')
Inputs may be any that keep to these rules, and one draw needn't show every extreme that they name: `a_matrix`: symmetric positive definite; its smallest eigenvalue is at least 1. `b_matrix`: symmetric positive definite; its smallest eigenvalue is at least 1.
All inputs are finite; a program needn't handle non-finite values. Where the computation divides by a largest or mean magnitude, that divisor is 1e-20 or more.
Results may differ from a plain program's by a relative error of at most 0.00012.
Values sent between devices are 32-bit elements; how exact they have to be, the bound alone decides.
No kernel may reach another device: no remote copies, remote signals or barrier semaphores. Data moves between devices by JAX's collectives and lax.ppermute only.
A program may use at most 128 MiB of HBM per device.

v0:
```python
import jax
import jax.numpy as jnp
from jax import lax
from jax.sharding import PartitionSpec as P

PANEL = 256
PIVOT_ITERS = 6
STEPS_A = 2
STEPS_B = 16
EXACT = lax.Precision.HIGHEST
CLOSE = lax.Precision.HIGH


def spread(value, axis, source):
    kept = jnp.where(lax.axis_index(axis) == source, value, 0).astype(value.dtype)
    return lax.psum(kept, axis)


def pivot_inverse(pivot):
    order = pivot.shape[0]
    unit_square = jnp.eye(order, dtype=jnp.float32)
    scaling = 1.0 / jnp.sqrt(jnp.sum(pivot * unit_square, axis=1))
    unit = pivot * scaling[:, None] * scaling[None, :]
    ceiling = jnp.max(jnp.sum(jnp.abs(unit), axis=1))
    approx = jnp.eye(order, dtype=jnp.float32) / ceiling
    for turn in range(PIVOT_ITERS):
        product = jnp.dot(unit, approx, precision=EXACT, preferred_element_type=jnp.float32)
        approx = 2.0 * approx - jnp.dot(
            approx, product, precision=EXACT, preferred_element_type=jnp.float32
        )
    return approx * scaling[:, None] * scaling[None, :]


def mul(left, right, dims, precision):
    return lax.dot_general(
        left, right, (dims, ((), ())), precision=precision, preferred_element_type=jnp.float32
    )


def sweep_panel(block, panel, places):
    order = block.shape[0]
    index = jnp.arange(order, dtype=jnp.int32)
    eye = (index[:, None] == jnp.concatenate([index, places])[None, :]).astype(jnp.float32)
    both = jnp.concatenate([block, panel], 1)
    for start in range(0, order, PANEL):
        stop = start + PANEL
        inverse = pivot_inverse(both[start:stop, start:stop].T)
        solved = mul(inverse, both[start:stop] - eye[start:stop], ((0,), (0,)), EXACT)
        updated = both - mul(both[:, start:stop], solved, ((1,), (0,)), CLOSE)
        both = jnp.concatenate([updated[:start], eye[start:stop] - solved, updated[stop:]], 0)
    return (both[:, order:], eye[:, order:])


def a_sweep(matrix, other):
    local_rows, local_cols = matrix.shape
    other_cols = other.shape[1]
    order = STEPS_A * PANEL
    row_place = lax.axis_index("row")
    col_place = lax.axis_index("col")
    panel = spread(matrix[:, :order], "col", 0)
    joined = spread(jnp.concatenate([matrix[:order], other[:order], panel[:order]], 1), "row", 0)
    rows = joined[:, : local_cols + other_cols]
    block = joined[:, local_cols + other_cols :].T
    places = row_place * local_rows + jnp.arange(local_rows, dtype=jnp.int32)
    swept, eye = sweep_panel(block, panel.T, places)
    solved = eye - swept
    new_matrix = matrix - mul(solved, rows[:, :local_cols], ((0,), (0,)), CLOSE)
    new_other = other - mul(solved, rows[:, local_cols:], ((0,), (0,)), CLOSE)
    front = jnp.where(col_place == 0, swept.T, new_matrix[:, :order])
    return (new_matrix.at[:, :order].set(front), new_other)


def b_sweep(matrix, row_count, col_count):
    local_rows, local_cols = matrix.shape
    order = min(local_rows, local_cols)
    steps = STEPS_B * PANEL // order
    row_part = order // row_count
    col_part = order // col_count
    row_place = lax.axis_index("row")
    col_place = lax.axis_index("col")
    dealt = matrix.T.reshape(local_cols // order, col_count, col_part, local_rows)
    dealt = lax.all_to_all(dealt, "col", 1, 0, tiled=True).reshape(local_cols, local_rows)
    dealt = dealt.T.reshape(local_rows // order, row_count, row_part, local_cols)
    dealt = lax.all_to_all(dealt, "row", 1, 0, tiled=True).reshape(local_rows, local_cols)
    index = jnp.arange(local_rows, dtype=jnp.int32)
    for step in range(steps):
        top = step * row_part
        left = step * col_part
        panel = lax.all_gather(dealt[:, left : left + col_part].T, "col", axis=0, tiled=True)
        joined = jnp.concatenate([dealt[top : top + row_part], panel[:, top : top + row_part].T], 1)
        joined = lax.all_gather(joined, "row", axis=0, tiled=True)
        rows = joined[:, :local_cols]
        block = joined[:, local_cols:].T
        inside = (index >= top) & (index < top + row_part)
        places = jnp.where(inside, index - top + row_place * row_part, -1)
        swept, eye = sweep_panel(block, panel, places)
        updated = dealt + mul(swept - eye, rows, ((0,), (0,)), CLOSE)
        own = lax.dynamic_slice_in_dim(swept, col_place * col_part, col_part, 0).T
        dealt = updated.at[:, left : left + col_part].set(own)
    back = dealt.reshape(steps, 1, row_part, local_cols)
    back = lax.all_to_all(back, "row", 0, 1, tiled=True).reshape(local_rows, local_cols)
    back = back.T.reshape(steps, 1, col_part, local_rows)
    back = lax.all_to_all(back, "col", 0, 1, tiled=True).reshape(local_cols, local_rows)
    return back.T


def solution(mesh):
    row_count = mesh.shape["row"]
    col_count = mesh.shape["col"]

    def body(a_matrix, b_matrix, c_matrix):
        b_local = jnp.sum(b_matrix * b_matrix)
        a_swept, c_swept = a_sweep(a_matrix, c_matrix)
        b_inverse = b_sweep(b_matrix, row_count, col_count)
        inv_local = jnp.sum(b_inverse * b_inverse)
        sums = lax.psum(jnp.stack([b_local, inv_local]), ("row", "col"))
        scale = jnp.sqrt(jnp.sqrt(sums[1] / sums[0]))
        b_next = 0.5 * (scale * b_matrix + b_inverse / scale)
        return (a_swept, c_swept, b_next)

    return jax.shard_map(
        body,
        mesh=mesh,
        in_specs=(P("row", "col"), P("row", "col"), P("row", "col")),
        out_specs=(P("row", "col"), P("row", "col"), P("row", "col")),
        check_vma=False,
    )
```

profile of v0, /device:TPU:10, one launch (start us, length us, event | category | flops | bytes accessed | tf_op | source)
XLA Modules:
  0.0 1504.4 jit_solution(638320156755108339)
XLA Ops:
  9.2 29.3 %all_to_all.48 = f32[1,8,64,1024]{3,2,0,1:T(8,128)} all-to-all(f32[1,8,64,1024]{3,2,0,1:T(8,128)S(1)} %bitcast.702), channel_id=1, replica_groups=mesh['row'=4,'col'=8] {'col'}, dimensions={1} | all-to-all | bytes 4194304 | tf_op jit(solution)/shard_map/all_to_all | solution.py:82
  40.6 51.6 %all_to_all.49 = f32[2,4,128,512]{3,2,0,1:T(8,128)S(1)} all-to-all(f32[2,4,128,512]{3,2,0,1:T(8,128)S(1)} %copy.155), channel_id=1, replica_groups=mesh['row'=4,'col'=8] {'row'}, dimensions={1} | all-to-all | bytes 4194304 | tf_op jit(solution)/shard_map/all_to_all | solution.py:84
  93.5 27.3 %all-gather.17.cloned.1.call-done = f32[512,1024]{1,0:T(8,128)} async-done(((f32[64,1024]{1,0:T(8,128)}), f32[512,1024]{1,0:T(8,128)}) %all-gather.17.cloned.1.call-update) | async-done | bytes 2097168 | tf_op jit(solution)/shard_map/all_gather | solution.py:89
  125.3 42.9 %all-gather.19.cloned.1.call-done = f32[512,1024]{1,0:T(8,128)} async-done(((f32[128,1024]{1,0:T(8,128)}), f32[512,1024]{1,0:T(8,128)}) %all-gather.19.cloned.1.call-update) | async-done | bytes 2097168 | tf_op jit(solution)/shard_map/all_gather | solution.py:91
  182.8 3.3 convolution_subtract_fusion.8
  203.7 3.9 fusion.123
  221.2 3.5 scatter.31
  227.9 27.0 %all-gather.21.cloned.1.call-done = f32[512,1024]{1,0:T(8,128)} async-done(((f32[64,1024]{1,0:T(8,128)}), f32[512,1024]{1,0:T(8,128)}) %all-gather.21.cloned.1.call-update) | async-done | bytes 2097168 | tf_op jit(solution)/shard_map/all_gather | solution.py:89
  258.9 43.4 %all-gather.23.cloned.1.call-done = f32[512,1024]{1,0:T(8,128)} async-done(((f32[128,1024]{1,0:T(8,128)}), f32[512,1024]{1,0:T(8,128)}) %all-gather.23.cloned.1.call-update) | async-done | bytes 2097168 | tf_op jit(solution)/shard_map/all_gather | solution.py:91
  316.9 3.3 convolution_subtract_fusion.7
  337.5 3.9 fusion.121
  355.2 3.9 scatter.34
  362.1 27.0 %all-gather.25.cloned.1.call-done = f32[512,1024]{1,0:T(8,128)} async-done(((f32[64,1024]{1,0:T(8,128)}), f32[512,1024]{1,0:T(8,128)}) %all-gather.25.cloned.1.call-update) | async-done | bytes 2097168 | tf_op jit(solution)/shard_map/all_gather | solution.py:89
  393.4 43.2 %all-gather.27.cloned.1.call-done = f32[512,1024]{1,0:T(8,128)} async-done(((f32[128,1024]{1,0:T(8,128)}), f32[512,1024]{1,0:T(8,128)}) %all-gather.27.cloned.1.call-update) | async-done | bytes 2097168 | tf_op jit(solution)/shard_map/all_gather | solution.py:91
  451.1 3.3 convolution_subtract_fusion.6
  471.7 3.9 fusion.119
  489.3 3.5 scatter.35
  495.9 27.0 %all-gather.29.cloned.1.call-done = f32[512,1024]{1,0:T(8,128)} async-done(((f32[64,1024]{1,0:T(8,128)}), f32[512,1024]{1,0:T(8,128)}) %all-gather.29.cloned.1.call-update) | async-done | bytes 2097168 | tf_op jit(solution)/shard_map/all_gather | solution.py:89
  527.0 43.3 %all-gather.31.cloned.1.call-done = f32[512,1024]{1,0:T(8,128)} async-done(((f32[128,1024]{1,0:T(8,128)}), f32[512,1024]{1,0:T(8,128)}) %all-gather.31.cloned.1.call-update) | async-done | bytes 2097168 | tf_op jit(solution)/shard_map/all_gather | solution.py:91
  584.9 3.3 convolution_subtract_fusion.5
  605.7 3.9 fusion.117
  623.4 3.9 scatter.36
  630.3 27.0 %all-gather.33.cloned.1.call-done = f32[512,1024]{1,0:T(8,128)} async-done(((f32[64,1024]{1,0:T(8,128)}), f32[512,1024]{1,0:T(8,128)}) %all-gather.33.cloned.1.call-update) | async-done | bytes 2097168 | tf_op jit(solution)/shard_map/all_gather | solution.py:89
  661.3 43.4 %all-gather.35.cloned.1.call-done = f32[512,1024]{1,0:T(8,128)} async-done(((f32[128,1024]{1,0:T(8,128)}), f32[512,1024]{1,0:T(8,128)}) %all-gather.35.cloned.1.call-update) | async-done | bytes 2097168 | tf_op jit(solution)/shard_map/all_gather | solution.py:91
  719.3 3.3 convolution_subtract_fusion.4
  739.9 3.9 fusion.115
  757.4 3.5 scatter.39
  764.1 27.0 %all-gather.37.cloned.1.call-done = f32[512,1024]{1,0:T(8,128)} async-done(((f32[64,1024]{1,0:T(8,128)}), f32[512,1024]{1,0:T(8,128)}) %all-gather.37.cloned.1.call-update) | async-done | bytes 2097168 | tf_op jit(solution)/shard_map/all_gather | solution.py:89
  795.3 43.2 %all-gather.39.cloned.1.call-done = f32[512,1024]{1,0:T(8,128)} async-done(((f32[128,1024]{1,0:T(8,128)}), f32[512,1024]{1,0:T(8,128)}) %all-gather.39.cloned.1.call-update) | async-done | bytes 2097168 | tf_op jit(solution)/shard_map/all_gather | solution.py:91
  853.1 3.3 convolution_subtract_fusion.3
  873.7 3.9 fusion.113
  891.3 3.9 scatter.40
  897.3 4.7 slice_select_fusion
  903.0 22.2 %all-gather.41.cloned.1.call-done = f32[512,1024]{1,0:T(8,128)} async-done(((f32[64,1024]{1,0:T(8,128)}), f32[512,1024]{1,0:T(8,128)}) %all-gather.41.cloned.1.call-update) | async-done | bytes 2097168 | tf_op jit(solution)/shard_map/all_gather | solution.py:89
  936.7 73.2 %all-reduce.3.cloned.1.call-done = f32[2048,512]{1,0:T(8,128)} async-done(((f32[2048,512]{1,0:T(8,128)}), f32[2048,512]{1,0:T(8,128)}) %all-reduce.3.cloned.1.call-update) | async-done | bytes 4194320 | tf_op jit(solution)/shard_map/psum | solution.py:16
  1011.7 3.6 maximum_select_fusion
  1015.8 39.9 %all-gather.43.cloned.1.call-done = f32[512,1024]{1,0:T(8,128)} async-done(((f32[128,1024]{1,0:T(8,128)}), f32[512,1024]{1,0:T(8,128)}) %all-gather.43.cloned.1.call-update) | async-done | bytes 2097168 | tf_op jit(solution)/shard_map/all_gather | solution.py:91
  1081.7 3.1 copy.207
  1090.9 3.9 fusion.111
  1097.8 3.5 slice_subtract_fusion.15
  1121.3 90.3 %all-reduce.5.cloned.1.call-done = f32[512,2048]{1,0:T(8,128)} async-done(((f32[512,2048]{1,0:T(8,128)}), f32[512,2048]{1,0:T(8,128)}) %all-reduce.5.cloned.1.call-update) | async-done | bytes 4194320 | tf_op jit(solution)/shard_map/psum | solution.py:16
  1223.5 18.7 %all-gather.45.cloned.1.call-done = f32[512,1024]{1,0:T(8,128)} async-done(((f32[64,1024]{1,0:T(8,128)}), f32[512,1024]{1,0:T(8,128)}) %all-gather.45.cloned.1.call-update) | async-done | bytes 2097168 | tf_op jit(solution)/shard_map/all_gather | solution.py:89
  1242.1 3.3 copy.213
  1251.4 7.1 fusion.13
  1270.0 22.7 %all-gather.47.cloned.1.call-done = f32[512,1024]{1,0:T(8,128)} async-done(((f32[128,1024]{1,0:T(8,128)}), f32[512,1024]{1,0:T(8,128)}) %all-gather.47.cloned.1.call-update) | async-done | bytes 2097168 | tf_op jit(solution)/shard_map/all_gather | solution.py:91
  1307.5 3.3 convolution_subtract_fusion.1
  1310.8 3.1 copy.215
  1328.2 3.9 fusion.109
  1341.9 3.2 fusion.53
  1345.1 3.4 scatter.44
  1348.6 6.7 all-to-all-start.2
  1356.6 3.3 copy.148
  1359.9 3.5 slice.808
  1367.4 7.8 fusion.15
  1375.2 3.4 copy.151
  1378.5 5.6 slice_subtract_fusion.3
  1385.7 4.6 fusion.234
  1390.3 9.9 all-to-all-done.2
  1403.9 5.1 all-to-all-start.3
  1409.1 3.0 slice_subtract_fusion.1
  1414.6 11.6 convolution_subtract_fusion
  1426.3 5.8 fusion.2
  1438.4 9.8 convolution_subtract_fusion.9
  1448.2 42.8 %psum.23 = f32[2]{0:T(128)S(1)} all-reduce(f32[2]{0:T(128)S(1)} %pad_maximum_fusion.35), channel_id=1, replica_groups=mesh['row'=4,'col'=8] {'row','col'}, use_global_device_ids=true, to_apply=%region_66.67 | all-reduce | flops 2 | bytes 16 | tf_op jit(solution)/shard_map/psum | solution.py:116
  (720 shorter events, 469.2 us)
Async XLA Ops:
  7.2 113.7 %all-gather.17.cloned.1.call-start = ((), (), s32[]{:S(2)}) async-start(), calls=%async_computation.6 | async-start | bytes 2359296 | tf_op jit(solution)/shard_map/all_gather | solution.py:89
  9.1 29.3 %copy-start.55 = (f32[1024,512]{0,1:T(8,128)}, f32[1024,512]{0,1:T(8,128)S(1)}, u32[]{:S(2)}) copy-start(f32[1024,512]{0,1:T(8,128)S(1)} %copy.152) | copy-start | bytes 6291460
  93.3 74.9 %all-gather.19.cloned.1.call-start = ((), (), s32[]{:S(2)}) async-start(), calls=%async_computation.7 | async-start | bytes 2621440 | tf_op jit(solution)/shard_map/all_gather | solution.py:91
  123.7 131.2 %all-gather.21.cloned.1.call-start = ((), (), s32[]{:S(2)}) async-start(), calls=%async_computation.8 | async-start | bytes 2359296 | tf_op jit(solution)/shard_map/all_gather | solution.py:89
  171.9 3.6 copy-start.21
  195.3 5.5 copy-start.12
  210.6 2.8 copy-start.88
  226.9 75.4 %all-gather.23.cloned.1.call-start = ((), (), s32[]{:S(2)}) async-start(), calls=%async_computation.9 | async-start | bytes 2621440 | tf_op jit(solution)/shard_map/all_gather | solution.py:91
  257.8 131.3 %all-gather.25.cloned.1.call-start = ((), (), s32[]{:S(2)}) async-start(), calls=%async_computation.10 | async-start | bytes 2359296 | tf_op jit(solution)/shard_map/all_gather | solution.py:89
  306.0 3.6 copy-start.23
  329.4 5.5 copy-start.13
  344.5 2.8 copy-start.89
  361.1 75.4 %all-gather.27.cloned.1.call-start = ((), (), s32[]{:S(2)}) async-start(), calls=%async_computation.11 | async-start | bytes 2621440 | tf_op jit(solution)/shard_map/all_gather | solution.py:91
  392.0 130.9 %all-gather.29.cloned.1.call-start = ((), (), s32[]{:S(2)}) async-start(), calls=%async_computation.12 | async-start | bytes 2359296 | tf_op jit(solution)/shard_map/all_gather | solution.py:89
  440.3 3.6 copy-start.25
  463.6 5.5 copy-start.14
  478.7 2.8 copy-start.90
  494.9 75.4 %all-gather.31.cloned.1.call-start = ((), (), s32[]{:S(2)}) async-start(), calls=%async_computation.13 | async-start | bytes 2621440 | tf_op jit(solution)/shard_map/all_gather | solution.py:91
  525.8 131.5 %all-gather.33.cloned.1.call-start = ((), (), s32[]{:S(2)}) async-start(), calls=%async_computation.14 | async-start | bytes 2359296 | tf_op jit(solution)/shard_map/all_gather | solution.py:89
  574.0 3.6 copy-start.27
  597.4 5.5 copy-start.15
  612.7 2.8 copy-start.91
  629.2 75.4 %all-gather.35.cloned.1.call-start = ((), (), s32[]{:S(2)}) async-start(), calls=%async_computation.15 | async-start | bytes 2621440 | tf_op jit(solution)/shard_map/all_gather | solution.py:91
  660.2 130.9 %all-gather.37.cloned.1.call-start = ((), (), s32[]{:S(2)}) async-start(), calls=%async_computation.16 | async-start | bytes 2359296 | tf_op jit(solution)/shard_map/all_gather | solution.py:89
  708.4 3.6 copy-start.29
  731.8 5.5 copy-start.16
  746.8 2.8 copy-start.92
  763.1 75.4 %all-gather.39.cloned.1.call-start = ((), (), s32[]{:S(2)}) async-start(), calls=%async_computation.17 | async-start | bytes 2621440 | tf_op jit(solution)/shard_map/all_gather | solution.py:91
  794.0 131.3 %all-gather.41.cloned.1.call-start = ((), (), s32[]{:S(2)}) async-start(), calls=%async_computation.18 | async-start | bytes 2359296 | tf_op jit(solution)/shard_map/all_gather | solution.py:89
  842.2 3.6 copy-start.31
  865.6 5.5 copy-start.17
  880.6 2.8 copy-start.93
  897.2 112.6 %all-reduce.3.cloned.1.call-start = ((), (), s32[]{:S(2)}) async-start(), calls=%async_computation.4 | async-start | bytes 8388608 | tf_op jit(solution)/shard_map/psum | solution.py:16
  902.0 153.7 %all-gather.43.cloned.1.call-start = ((), (), s32[]{:S(2)}) async-start(), calls=%async_computation.19 | async-start | bytes 2621440 | tf_op jit(solution)/shard_map/all_gather | solution.py:91
  928.1 283.5 %all-reduce.5.cloned.1.call-start = ((), (), s32[]{:S(2)}) async-start(), calls=%async_computation.5 | async-start | bytes 8388608 | tf_op jit(solution)/shard_map/psum | solution.py:16
  928.7 5.8 copy-start.107
  1015.3 226.8 %all-gather.45.cloned.1.call-start = ((), (), s32[]{:S(2)}) async-start(), calls=%async_computation.20 | async-start | bytes 2359296 | tf_op jit(solution)/shard_map/all_gather | solution.py:89
  1059.5 3.6 copy-start.33
  1063.5 2.9 copy-start.43
  1064.4 2.5 copy-start
  1084.8 4.5 copy-start.19
  1087.6 3.3 copy-start.1
  1097.8 3.5 copy-start.85
  1097.8 3.8 copy-start.94
  1103.1 2.6 copy-start.66
  1117.7 174.9 %all-gather.47.cloned.1.call-start = ((), (), s32[]{:S(2)}) async-start(), calls=%async_computation.21 | async-start | bytes 2621440 | tf_op jit(solution)/shard_map/all_gather | solution.py:91
  1215.4 3.6 copy-start.38
  1248.2 3.2 copy-start.39
  1251.4 7.1 copy-start.36
  1296.4 3.8 copy-start.35
  1320.1 5.5 copy-start.11
  1335.1 2.8 copy-start.87
  1348.6 51.7 %all-to-all-start.2 = ((f32[8,1,128,512]{3,2,1,0:T(8,128)}), f32[8,1,128,512]{3,2,1,0:T(8,128)}, u32[]{:S(2)}, u32[]{:S(2)}) async-start(f32[8,1,128,512]{3,2,1,0:T(8,128)} %bitcast.706), calls=%async_computation.2 | async-start | bytes 4194304 | tf_op jit(solution)/shard_map/all_to_all | solution.py:101
  1356.6 10.8 slice-start
  1359.9 7.5 slice-start.1
  1375.2 3.4 copy-start.97
  1378.5 7.2 copy-start.7
  1378.5 7.2 copy-start.8
  1403.9 8.2 slice-start.2
  1403.9 30.3 %all-to-all-start.3 = ((f32[8,1,64,1024]{3,2,1,0:T(8,128)}), f32[8,1,64,1024]{3,2,1,0:T(8,128)}, u32[]{:S(2)}, u32[]{:S(2)}) async-start(f32[8,1,64,1024]{3,2,1,0:T(8,128)} %bitcast.72), calls=%async_computation.3 | async-start | bytes 4194304 | tf_op jit(solution)/shard_map/all_to_all | solution.py:103
  1409.1 3.8 slice-start.3
  1409.1 5.5 copy-start.4
  1412.2 14.1 copy-start.3
  1426.3 12.1 copy-start.5
  (69 other events, 118.0 us)
Sparse Core Ops, SparseCore 0:
  93.5 27.2 all-gather.16
  123.8 44.3 all-gather.18
  227.0 27.8 all-gather.20
  257.9 44.3 all-gather.22
  361.2 27.8 all-gather.24
  392.2 44.3 all-gather.26
  495.0 27.8 all-gather.28
  525.9 44.3 all-gather.30
  629.4 27.8 all-gather.32
  660.3 44.3 all-gather.34
  763.2 27.8 all-gather.36
  794.1 44.3 all-gather.38
  897.3 27.8 all-gather.40
  928.9 80.8 all-reduce.2
  1011.2 44.4 all-gather.42
  1058.5 153.1 all-reduce.4
  1213.4 28.6 all-gather.44
  1248.3 44.3 all-gather.46
where the time goes:
time: 1520 us; the launch traced here: 1500 us
  waiting for transfers between devices  701 us (46%)
  matrix products  290 us (19%)
  local copies, waits for them, and re-layouts  229 us (15%)
  blocking collectives  124 us (8%)
  other arithmetic  115 us (8%)
  between operations  31.5 us (2%)
    all_gather x8, waiting for transfers between devices, b_sweep(): joined = lax.all_gather(joined, 'row', axis=0, tiled=True)  322 us
    all_gather x8, waiting for transfers between devices, b_sweep(): lax.all_gather(dealt[:, left:left + col_part].T, 'col', axis=0, tiled=True)  203 us
    psum x2, waiting for transfers between devices, spread(): return lax.psum(kept, axis)  163 us
    dot_general x46, matrix products, mul(): lax.dot_general(left, right, (dims, ((), ())), precision=precision, prefe...  149 us
    dot_general x108, matrix products, pivot_inverse(): jnp.dot(unit, approx, precision=EXACT, preferred_element_type=jnp.float32)  97.6 us
    unnamed x226, local copies, waits for them, and re-layouts  55.5 us
    dot_general x18, local copies, waits for them, and re-layouts, mul(): lax.dot_general(left, right, (dims, ((), ())), precision=precision, prefe...  55.2 us
    all_to_all x1, blocking collectives, b_sweep(): lax.all_to_all(dealt, 'row', 1, 0, tiled=True)  51.6 us
  transfers between devices with their start and end apart: 20, of which 20 were waited for; matrix products, arithmetic and copies ran while one was open for 12% of the time, Pallas kernels for 0%

commit v1 on v0

--- a/solution.py
+++ b/solution.py
@@ -13,7 +13,7 @@
 
 def spread(value, axis, source):
     kept = jnp.where(lax.axis_index(axis) == source, value, 0).astype(value.dtype)
-    return lax.psum(kept, axis)
+    return jnp.sum(lax.all_gather(kept, axis), axis=0)
 
 
 def pivot_inverse(pivot):

time: 1520 us -> 1700 us (1.12)
  blocking collectives: 124 us -> 248 us
  waiting for transfers between devices: 701 us -> 783 us
  local copies, waits for them, and re-layouts: 229 us -> 207 us
    all_gather x0 -> x2, waiting for transfers between devices: none -> 225 us  [spread(): return jnp.sum(lax.all_gather(kept, axis), axis=0)]
    psum x2 -> x0, waiting for transfers between devices: 163 us -> none  [spread(): return lax.psum(kept, axis)]
    all_to_all x0 -> x1, blocking collectives: none -> 107 us  [b_sweep(): lax.all_to_all(back, 'row', 0, 1, tiled=True)]
    reduce_sum x0 -> x2, other arithmetic: none -> 25.6 us  [spread(): return jnp.sum(lax.all_gather(kept, axis), axis=0)]
    psum x1, blocking collectives: 42.8 us -> 60.2 us  [body(): sums = lax.psum(jnp.stack([b_local, inv_local]), ('row', 'col'))]
    all_to_all x1, waiting for transfers between devices: 2.22 us -> 19.4 us  [b_sweep(): lax.all_to_all(back, 'col', 0, 1, tiled=True)]
    unnamed x226 -> x214, local copies, waits for them, and re-layouts: 55.5 us -> 50.3 us
  transfers between devices with their start and end apart: 20 -> 19, of which waited for: 20 -> 19; matrix products, arithmetic and copies ran while one was open for 12% -> 7% of each run, Pallas kernels for 0% -> 0%
where the time goes in v1:
time: 1700 us; the launch traced here: 1680 us
  waiting for transfers between devices  783 us (46%)
  matrix products  297 us (17%)
  blocking collectives  248 us (15%)
  local copies, waits for them, and re-layouts  207 us (12%)
  other arithmetic  113 us (7%)
  between operations  32.2 us (2%)
    all_gather x8, waiting for transfers between devices, b_sweep(): joined = lax.all_gather(joined, 'row', axis=0, tiled=True)  327 us
    all_gather x2, waiting for transfers between devices, spread(): return jnp.sum(lax.all_gather(kept, axis), axis=0)  225 us
    all_gather x8, waiting for transfers between devices, b_sweep(): lax.all_gather(dealt[:, left:left + col_part].T, 'col', axis=0, tiled=True)  212 us
    dot_general x46, matrix products, mul(): lax.dot_general(left, right, (dims, ((), ())), precision=precision, prefe...  163 us
    all_to_all x1, blocking collectives, b_sweep(): lax.all_to_all(back, 'row', 0, 1, tiled=True)  107 us
    dot_general x108, matrix products, pivot_inverse(): jnp.dot(unit, approx, precision=EXACT, preferred_element_type=jnp.float32)  92.9 us
    psum x1, blocking collectives, body(): sums = lax.psum(jnp.stack([b_local, inv_local]), ('row', 'col'))  60.2 us
    dot_general x18, local copies, waits for them, and re-layouts, mul(): lax.dot_general(left, right, (dims, ((), ())), precision=precision, prefe...  54.4 us
  transfers between devices with their start and end apart: 19, of which 19 were waited for; matrix products, arithmetic and copies ran while one was open for 7% of the time, Pallas kernels for 0%

profile of v1, /device:TPU:10, one launch (start us, length us, event | category | flops | bytes accessed | tf_op | source)
XLA Modules:
  0.0 1684.9 jit_solution(6761721501892296788)
XLA Ops:
  9.2 29.3 %all_to_all.48 = f32[1,8,64,1024]{3,2,0,1:T(8,128)} all-to-all(f32[1,8,64,1024]{3,2,0,1:T(8,128)S(1)} %bitcast.712), channel_id=1, replica_groups=mesh['row'=4,'col'=8] {'col'}, dimensions={1} | all-to-all | bytes 4194304 | tf_op jit(solution)/shard_map/all_to_all | solution.py:82
  40.6 51.6 %all_to_all.49 = f32[2,4,128,512]{3,2,0,1:T(8,128)S(1)} all-to-all(f32[2,4,128,512]{3,2,0,1:T(8,128)S(1)} %copy.155), channel_id=1, replica_groups=mesh['row'=4,'col'=8] {'row'}, dimensions={1} | all-to-all | bytes 4194304 | tf_op jit(solution)/shard_map/all_to_all | solution.py:84
  93.5 27.3 %all-gather.22.cloned.1.call-done = f32[512,1024]{1,0:T(8,128)} async-done(((f32[64,1024]{1,0:T(8,128)}), f32[512,1024]{1,0:T(8,128)}) %all-gather.22.cloned.1.call-update) | async-done | bytes 2097168 | tf_op jit(solution)/shard_map/all_gather | solution.py:89
  125.5 42.8 %all-gather.24.cloned.1.call-done = f32[512,1024]{1,0:T(8,128)} async-done(((f32[128,1024]{1,0:T(8,128)}), f32[512,1024]{1,0:T(8,128)}) %all-gather.24.cloned.1.call-update) | async-done | bytes 2097168 | tf_op jit(solution)/shard_map/all_gather | solution.py:91
  178.9 3.9 fusion.107
  185.8 4.1 convolution_subtract_fusion.8
  201.9 3.9 fusion.123
  219.6 3.5 scatter.31
  226.3 27.0 %all-gather.26.cloned.1.call-done = f32[512,1024]{1,0:T(8,128)} async-done(((f32[64,1024]{1,0:T(8,128)}), f32[512,1024]{1,0:T(8,128)}) %all-gather.26.cloned.1.call-update) | async-done | bytes 2097168 | tf_op jit(solution)/shard_map/all_gather | solution.py:89
  257.4 43.3 %all-gather.28.cloned.1.call-done = f32[512,1024]{1,0:T(8,128)} async-done(((f32[128,1024]{1,0:T(8,128)}), f32[512,1024]{1,0:T(8,128)}) %all-gather.28.cloned.1.call-update) | async-done | bytes 2097168 | tf_op jit(solution)/shard_map/all_gather | solution.py:91
  311.3 3.9 fusion.103
  318.3 4.1 convolution_subtract_fusion.7
  334.2 3.9 fusion.121
  352.0 3.9 scatter.34
  358.9 27.0 %all-gather.30.cloned.1.call-done = f32[512,1024]{1,0:T(8,128)} async-done(((f32[64,1024]{1,0:T(8,128)}), f32[512,1024]{1,0:T(8,128)}) %all-gather.30.cloned.1.call-update) | async-done | bytes 2097168 | tf_op jit(solution)/shard_map/all_gather | solution.py:89
  390.3 43.0 %all-gather.32.cloned.1.call-done = f32[512,1024]{1,0:T(8,128)} async-done(((f32[128,1024]{1,0:T(8,128)}), f32[512,1024]{1,0:T(8,128)}) %all-gather.32.cloned.1.call-update) | async-done | bytes 2097168 | tf_op jit(solution)/shard_map/all_gather | solution.py:91
  444.0 3.9 fusion.99
  451.0 4.1 convolution_subtract_fusion.6
  466.8 3.9 fusion.119
  484.5 3.5 scatter.35
  491.1 27.0 %all-gather.34.cloned.1.call-done = f32[512,1024]{1,0:T(8,128)} async-done(((f32[64,1024]{1,0:T(8,128)}), f32[512,1024]{1,0:T(8,128)}) %all-gather.34.cloned.1.call-update) | async-done | bytes 2097168 | tf_op jit(solution)/shard_map/all_gather | solution.py:89
  522.3 43.2 %all-gather.36.cloned.1.call-done = f32[512,1024]{1,0:T(8,128)} async-done(((f32[128,1024]{1,0:T(8,128)}), f32[512,1024]{1,0:T(8,128)}) %all-gather.36.cloned.1.call-update) | async-done | bytes 2097168 | tf_op jit(solution)/shard_map/all_gather | solution.py:91
  576.2 3.9 fusion.95
  583.2 4.1 convolution_subtract_fusion.5
  599.3 3.9 fusion.117
  617.1 3.9 scatter.36
  623.9 27.0 %all-gather.38.cloned.1.call-done = f32[512,1024]{1,0:T(8,128)} async-done(((f32[64,1024]{1,0:T(8,128)}), f32[512,1024]{1,0:T(8,128)}) %all-gather.38.cloned.1.call-update) | async-done | bytes 2097168 | tf_op jit(solution)/shard_map/all_gather | solution.py:89
  655.1 43.3 %all-gather.40.cloned.1.call-done = f32[512,1024]{1,0:T(8,128)} async-done(((f32[128,1024]{1,0:T(8,128)}), f32[512,1024]{1,0:T(8,128)}) %all-gather.40.cloned.1.call-update) | async-done | bytes 2097168 | tf_op jit(solution)/shard_map/all_gather | solution.py:91
  709.0 3.9 fusion.91
  716.0 4.1 convolution_subtract_fusion.4
  731.9 3.9 fusion.115
  749.5 3.5 scatter.39
  756.2 27.0 %all-gather.42.cloned.1.call-done = f32[512,1024]{1,0:T(8,128)} async-done(((f32[64,1024]{1,0:T(8,128)}), f32[512,1024]{1,0:T(8,128)}) %all-gather.42.cloned.1.call-update) | async-done | bytes 2097168 | tf_op jit(solution)/shard_map/all_gather | solution.py:89
  787.6 43.0 %all-gather.44.cloned.1.call-done = f32[512,1024]{1,0:T(8,128)} async-done(((f32[128,1024]{1,0:T(8,128)}), f32[512,1024]{1,0:T(8,128)}) %all-gather.44.cloned.1.call-update) | async-done | bytes 2097168 | tf_op jit(solution)/shard_map/all_gather | solution.py:91
  841.3 3.9 fusion.87
  848.2 4.1 convolution_subtract_fusion.3
  864.1 3.9 fusion.113
  881.9 3.9 scatter.40
  888.8 27.0 %all-gather.46.cloned.1.call-done = f32[512,1024]{1,0:T(8,128)} async-done(((f32[64,1024]{1,0:T(8,128)}), f32[512,1024]{1,0:T(8,128)}) %all-gather.46.cloned.1.call-update) | async-done | bytes 2097168 | tf_op jit(solution)/shard_map/all_gather | solution.py:89
  919.9 43.3 %all-gather.48.cloned.1.call-done = f32[512,1024]{1,0:T(8,128)} async-done(((f32[128,1024]{1,0:T(8,128)}), f32[512,1024]{1,0:T(8,128)}) %all-gather.48.cloned.1.call-update) | async-done | bytes 2097168 | tf_op jit(solution)/shard_map/all_gather | solution.py:91
  973.8 3.9 fusion.83
  980.8 4.1 convolution_subtract_fusion.2
  996.9 3.9 fusion.111
  1019.6 4.7 slice_select_fusion
  1025.3 22.3 %all-gather.50.cloned.1.call-done = f32[512,1024]{1,0:T(8,128)} async-done(((f32[64,1024]{1,0:T(8,128)}), f32[512,1024]{1,0:T(8,128)}) %all-gather.50.cloned.1.call-update) | async-done | bytes 2097168 | tf_op jit(solution)/shard_map/all_gather | solution.py:89
  1053.7 156.9 %all-gather.54.cloned.1.call-done = f32[16384,512]{1,0:T(8,128)} async-done(((f32[2048,512]{1,0:T(8,128)}), f32[16384,512]{1,0:T(8,128)}) %all-gather.54.cloned.1.call-update) | async-done | bytes 33554448 | tf_op jit(solution)/shard_map/all_gather | solution.py:16
  1210.6 15.5 reduce_sum.360
  1231.6 24.8 %all-gather.52.cloned.1.call-done = f32[512,1024]{1,0:T(8,128)} async-done(((f32[128,1024]{1,0:T(8,128)}), f32[512,1024]{1,0:T(8,128)}) %all-gather.52.cloned.1.call-update) | async-done | bytes 2097168 | tf_op jit(solution)/shard_map/all_gather | solution.py:91
  1267.1 3.9 fusion.79
  1274.3 4.6 convolution_subtract_fusion.1
  1290.9 3.9 fusion.109
  1311.3 106.8 %all_to_all.50 = f32[8,1,128,512]{3,2,1,0:T(8,128)S(1)} all-to-all(f32[8,1,128,512]{3,2,1,0:T(8,128)} %bitcast.716), channel_id=1, replica_groups=mesh['row'=4,'col'=8] {'row'}, dimensions={0} | all-to-all | bytes 4194304 | tf_op jit(solution)/shard_map/all_to_all | solution.py:101
  1420.2 4.2 all-to-all-start.3
  1430.1 19.4 %all-to-all-done.3 = f32[8,1,64,1024]{3,2,1,0:T(8,128)S(1)} async-done(((f32[8,1,64,1024]{3,2,1,0:T(8,128)}), f32[8,1,64,1024]{3,2,1,0:T(8,128)S(1)}, u32[]{:S(2)}, u32[]{:S(2)}) %all-to-all-start.3) | async-done | bytes 2097184 | tf_op jit(solution)/shard_map/all_to_all | solution.py:103
  1452.6 60.2 %psum.7 = f32[2]{0:T(128)S(1)} all-reduce(f32[2]{0:T(128)S(1)} %pad_maximum_fusion.35), channel_id=1, replica_groups=mesh['row'=4,'col'=8] {'row','col'}, use_global_device_ids=true, to_apply=%region_66.67 | all-reduce | flops 2 | bytes 16 | tf_op jit(solution)/shard_map/psum | solution.py:116
  1518.8 67.8 %all-gather.20.cloned.1.call-done = f32[4,512,2048]{2,1,0:T(8,128)} async-done(((f32[1,512,2048]{2,1,0:T(8,128)}), f32[4,512,2048]{2,1,0:T(8,128)}) %all-gather.20.cloned.1.call-update) | async-done | bytes 16777232 | tf_op jit(solution)/shard_map/all_gather | solution.py:16
  1586.5 10.1 reduce_sum.361
  1604.6 6.5 fusion.13
  1613.4 5.0 fusion
  1633.8 7.8 fusion.15
  1641.5 3.5 copy.151
  1645.0 4.9 slice_subtract_fusion.3
  1654.7 10.5 convolution_subtract_fusion
  1665.3 7.0 convolution_subtract_fusion.9
  (708 shorter events, 424.4 us)
Async XLA Ops:
  7.2 113.7 %all-gather.22.cloned.1.call-start = ((), (), s32[]{:S(2)}) async-start(), calls=%async_computation.5 | async-start | bytes 2359296 | tf_op jit(solution)/shard_map/all_gather | solution.py:89
  9.1 29.3 %copy-start.55 = (f32[1024,512]{0,1:T(8,128)}, f32[1024,512]{0,1:T(8,128)S(1)}, u32[]{:S(2)}) copy-start(f32[1024,512]{0,1:T(8,128)S(1)} %copy.152) | copy-start | bytes 6291460
  93.4 74.9 %all-gather.24.cloned.1.call-start = ((), (), s32[]{:S(2)}) async-start(), calls=%async_computation.6 | async-start | bytes 2621440 | tf_op jit(solution)/shard_map/all_gather | solution.py:91
  123.7 129.5 %all-gather.26.cloned.1.call-start = ((), (), s32[]{:S(2)}) async-start(), calls=%async_computation.7 | async-start | bytes 2359296 | tf_op jit(solution)/shard_map/all_gather | solution.py:89
  172.0 3.6 copy-start.21
  193.6 5.8 copy-start.5
  208.8 2.5 copy-start.71
  208.8 2.8 copy-start.80
  225.2 75.5 %all-gather.28.cloned.1.call-start = ((), (), s32[]{:S(2)}) async-start(), calls=%async_computation.8 | async-start | bytes 2621440 | tf_op jit(solution)/shard_map/all_gather | solution.py:91
  256.2 129.8 %all-gather.30.cloned.1.call-start = ((), (), s32[]{:S(2)}) async-start(), calls=%async_computation.9 | async-start | bytes 2359296 | tf_op jit(solution)/shard_map/all_gather | solution.py:89
  304.4 3.6 copy-start.23
  326.1 5.5 copy-start.7
  341.1 2.5 copy-start.72
  341.1 2.8 copy-start.81
  357.9 75.5 %all-gather.32.cloned.1.call-start = ((), (), s32[]{:S(2)}) async-start(), calls=%async_computation.10 | async-start | bytes 2621440 | tf_op jit(solution)/shard_map/all_gather | solution.py:91
  388.9 129.3 %all-gather.34.cloned.1.call-start = ((), (), s32[]{:S(2)}) async-start(), calls=%async_computation.11 | async-start | bytes 2359296 | tf_op jit(solution)/shard_map/all_gather | solution.py:89
  437.1 3.6 copy-start.25
  458.8 5.5 copy-start.9
  473.8 2.5 copy-start.73
  473.8 2.8 copy-start.82
  490.1 75.5 %all-gather.36.cloned.1.call-start = ((), (), s32[]{:S(2)}) async-start(), calls=%async_computation.12 | async-start | bytes 2621440 | tf_op jit(solution)/shard_map/all_gather | solution.py:91
  521.1 129.9 %all-gather.38.cloned.1.call-start = ((), (), s32[]{:S(2)}) async-start(), calls=%async_computation.13 | async-start | bytes 2359296 | tf_op jit(solution)/shard_map/all_gather | solution.py:89
  569.3 3.6 copy-start.27
  591.0 5.5 copy-start.11
  606.2 2.5 copy-start.74
  606.2 2.8 copy-start.83
  622.9 75.4 %all-gather.40.cloned.1.call-start = ((), (), s32[]{:S(2)}) async-start(), calls=%async_computation.14 | async-start | bytes 2621440 | tf_op jit(solution)/shard_map/all_gather | solution.py:91
  653.9 129.3 %all-gather.42.cloned.1.call-start = ((), (), s32[]{:S(2)}) async-start(), calls=%async_computation.15 | async-start | bytes 2359296 | tf_op jit(solution)/shard_map/all_gather | solution.py:89
  702.1 3.6 copy-start.29
  723.8 5.5 copy-start.13
  738.8 2.5 copy-start.75
  738.8 2.8 copy-start.84
  755.2 75.5 %all-gather.44.cloned.1.call-start = ((), (), s32[]{:S(2)}) async-start(), calls=%async_computation.16 | async-start | bytes 2621440 | tf_op jit(solution)/shard_map/all_gather | solution.py:91
  786.1 129.7 %all-gather.46.cloned.1.call-start = ((), (), s32[]{:S(2)}) async-start(), calls=%async_computation.17 | async-start | bytes 2359296 | tf_op jit(solution)/shard_map/all_gather | solution.py:89
  834.4 3.6 copy-start.31
  856.0 5.5 copy-start.15
  871.0 2.8 copy-start.85
  887.7 75.4 %all-gather.48.cloned.1.call-start = ((), (), s32[]{:S(2)}) async-start(), calls=%async_computation.18 | async-start | bytes 2621440 | tf_op jit(solution)/shard_map/all_gather | solution.py:91
  918.7 128.9 %all-gather.50.cloned.1.call-start = ((), (), s32[]{:S(2)}) async-start(), calls=%async_computation.19 | async-start | bytes 2359296 | tf_op jit(solution)/shard_map/all_gather | solution.py:89
  966.9 3.6 copy-start.33
  988.6 5.5 copy-start.17
  1003.9 2.8 copy-start.86
  1019.5 191.1 %all-gather.54.cloned.1.call-start = ((), (), s32[]{:S(2)}) async-start(), calls=%async_computation.21 | async-start | bytes 37748736 | tf_op jit(solution)/shard_map/all_gather | solution.py:16
  1024.3 232.1 %all-gather.52.cloned.1.call-start = ((), (), s32[]{:S(2)}) async-start(), calls=%async_computation.20 | async-start | bytes 2621440 | tf_op jit(solution)/shard_map/all_gather | solution.py:91
  1049.5 4.2 copy-start.39
  1050.5 536.0 %all-gather.20.cloned.1.call-start = ((), (), s32[]{:S(2)}) async-start(), calls=%async_computation.4 | async-start | bytes 20971520 | tf_op jit(solution)/shard_map/all_gather | solution.py:16
  1260.2 3.6 copy-start.35
  1282.6 5.9 copy-start.19
  1297.8 2.5 copy-start.78
  1297.8 2.9 copy-start.79
  1420.2 29.3 %all-to-all-start.3 = ((f32[8,1,64,1024]{3,2,1,0:T(8,128)}), f32[8,1,64,1024]{3,2,1,0:T(8,128)S(1)}, u32[]{:S(2)}, u32[]{:S(2)}) async-start(f32[8,1,64,1024]{3,2,1,0:T(8,128)} %bitcast.717), calls=%async_computation.3 | async-start | bytes 4194304 | tf_op jit(solution)/shard_map/all_to_all | solution.py:103
  1597.9 5.8 copy-start.36
  1602.1 2.5 copy-start
  1618.4 3.1 copy-start.1
  1618.5 15.2 slice-start
  1624.7 9.0 slice-start.1
  1645.0 5.0 copy-start.2
  1645.0 5.6 copy-start.3
  1645.0 8.4 slice-start.2
  1645.0 8.4 slice-start.4
  1650.6 2.9 slice-start.3
  1650.6 4.1 slice-start.5
  1665.3 7.0 copy-start.53
  1674.2 3.4 copy-start.54
  (61 other events, 108.3 us)
Sparse Core Ops, SparseCore 0:
  93.5 27.2 all-gather.21
  123.9 44.3 all-gather.23
  225.4 27.8 all-gather.25
  256.3 44.3 all-gather.27
  358.0 27.8 all-gather.29
  389.0 44.3 all-gather.31
  490.2 27.8 all-gather.33
  521.2 44.3 all-gather.35
  623.0 27.8 all-gather.37
  654.0 44.3 all-gather.39
  755.3 27.8 all-gather.41
  786.2 44.3 all-gather.43
  887.9 27.8 all-gather.45
  918.8 44.3 all-gather.47
  1019.7 27.9 all-gather.49
  1049.9 160.6 all-gather.53
  1212.0 44.3 all-gather.51
  1257.8 328.6 all-gather.19
